TPU v7x, 32 devices: a whole 2x2x4 slice. The times are simulated.
32 devices in a mesh: groups: 2 (over y), band: 4 (over z), chan: 4 (over x, core).
Axes of the slice: x: 2, y: 2, z: 4, core: 2. Of those that a mesh axis runs over, the one named last changes fastest.
Arguments:
- slide_region: float32 [16, 32, 8192], P('chan', ('groups', 'band')), parts along dimension 1, may hold values from -6 to 6
- row_taps: float32 [16, 257], P('chan'), may hold values from -0.375 to 0.375
- column_taps: float32 [16, 257], replicated, may hold values from -0.375 to 0.375
- channel_mix: float32 [16, 16], replicated, may hold values from -1.5 to 1.5
Outputs:
- filtered: float32 [16, 32, 8192], P('chan', ('groups', 'band')), parts along dimension 1
There are 2 independent parts, one for each index of `groups`. A program takes and returns all parts, laid end to end along the dimension named above; an argument that names none is the same for every part. Nothing has to cross between parts.
All inputs are finite; a program needn't handle non-finite values.
Results may differ from a plain program's by a relative error of at most 0.00007.
Values sent between devices are 32-bit elements; how exact they have to be, the bound alone decides.
A program may use at most 64 MiB of HBM per device.

v0:
```python
import jax
import jax.numpy as jnp
from jax import lax
from jax.sharding import PartitionSpec as P

precise = lax.Precision.HIGHEST


def band_tables(filter_taps, tile_size):
    channels, length = filter_taps.shape
    margin = (length - 1) // 2
    period = 4 * tile_size
    border = 3 * tile_size + length
    widened = jnp.pad(filter_taps, ((0, 0), (border, border)))
    lowest = margin - tile_size + border
    window = widened[:, lowest : lowest + 3 * tile_size]
    vector = jnp.pad(window, ((0, 0), (0, tile_size)))
    repeated = jnp.tile(vector, (1, tile_size))[:, : tile_size * (period - 1)]
    toeplitz = repeated.reshape(channels, tile_size, period - 1)[:, :, : 3 * tile_size]
    stacked = jnp.transpose(toeplitz, (0, 2, 1))
    return stacked.reshape(channels, 3, tile_size, tile_size)


def along_columns(signal, filter_taps):
    tile_size = 128
    tables = band_tables(filter_taps, tile_size)
    channels, row_count, col_count = signal.shape
    tile_count = col_count // tile_size
    tiled = signal.reshape(channels, row_count, tile_count, tile_size)
    padded = jnp.pad(tiled, ((0, 0), (0, 0), (1, 1), (0, 0)))
    result = jnp.einsum(
        "crti,cij->crtj", padded[:, :, 0:tile_count], tables[:, 0], precision=precise
    )
    result = result + jnp.einsum(
        "crti,cij->crtj", padded[:, :, 1 : tile_count + 1], tables[:, 1], precision=precise
    )
    result = result + jnp.einsum(
        "crti,cij->crtj", padded[:, :, 2:], tables[:, 2], precision=precise
    )
    return result.reshape(channels, row_count, col_count)


def along_rows(signal, filter_taps):
    channels, row_count, col_count = signal.shape
    tile_size = 128 if row_count % 128 == 0 else row_count
    tables = band_tables(filter_taps, tile_size)
    tile_count = row_count // tile_size
    tiled = signal.reshape(channels, tile_count, tile_size, col_count)
    padded = jnp.pad(tiled, ((0, 0), (1, 1), (0, 0), (0, 0)))
    result = jnp.einsum("ctiw,cij->ctjw", padded[:, 0:tile_count], tables[:, 0], precision=precise)
    result = result + jnp.einsum(
        "ctiw,cij->ctjw", padded[:, 1 : tile_count + 1], tables[:, 1], precision=precise
    )
    result = result + jnp.einsum("ctiw,cij->ctjw", padded[:, 2:], tables[:, 2], precision=precise)
    return result.reshape(channels, row_count, col_count)


def on_device(slide_region, row_taps, column_taps, channel_mix):
    local_channels = slide_region.shape[0]
    across = along_columns(slide_region, row_taps)
    column_band = lax.all_to_all(across, "band", split_axis=2, concat_axis=1, tiled=True)
    first_channel = lax.axis_index("chan") * local_channels
    own_taps = lax.dynamic_slice_in_dim(column_taps, first_channel, local_channels, 0)
    vertical = along_rows(column_band, own_taps)
    own_mixing = lax.dynamic_slice_in_dim(channel_mix, first_channel, local_channels, 0)
    blended = jnp.einsum(
        "oc,chw->ohw",
        own_mixing,
        lax.all_gather(vertical, "chan", axis=0, tiled=True),
        precision=precise,
    )
    return lax.all_to_all(blended, "band", split_axis=1, concat_axis=2, tiled=True)


def solution(mesh):
    in_specs = (P("chan", ("groups", "band"), None), P("chan", None), P(), P())
    out_specs = P("chan", ("groups", "band"), None)
    return jax.shard_map(
        on_device, mesh=mesh, in_specs=in_specs, out_specs=out_specs, check_vma=False
    )
```

profile of v0, /device:TPU:0, one launch (start us, length us, event | category | flops | bytes accessed | tf_op | source)
XLA Modules:
  0.0 165.2 jit_solution(12233661536541176305)
XLA Ops:
  6.5 0.0 copy-start
  6.5 0.7 pad_slice_fusion.4
  7.3 0.1 broadcast_bitcast_fusion
  7.4 0.7 copy.47
  8.1 0.1 slice.68
  8.1 0.0 copy-start.1
  8.2 1.0 reshape.47
  9.2 0.1 slice_bitcast_fusion
  9.2 0.3 copy.24
  9.5 0.0 copy-done.1
  9.5 0.4 reshape.46
  9.9 0.6 fusion.4
  10.5 0.6 fusion.5
  11.2 0.6 fusion.3
  11.8 8.6 %copy.38 = f32[4,4,64,128]{1,0,3,2:T(4,128)} copy(f32[4,4,64,128]{3,2,1,0:T(8,128)S(1)} %fusion.3) | data formatting | bytes 1048576 | tf_op jit(solution)/shard_map/reshape | solution.py:40
  20.4 24.6 %reshape.55 = f32[4,1,32768]{2,1,0:T(1,128)} reshape(f32[8192,4,4]{2,1,0:T(4,128)} %bitcast.68) | data formatting | bytes 1048576
  45.0 6.3 %all-to-all-start = ((f32[4,1,32768]{2,1,0:T(1,128)}), f32[4,1,32768]{2,1,0:T(1,128)S(1)}, u32[]{:S(2)}, u32[]{:S(2)}) async-start(f32[4,1,32768]{2,1,0:T(1,128)} %reshape.55), calls=%async_computation | async-start | bytes 1048576 | tf_op jit(solution)/shard_map/all_to_all | solution.py:61
  51.3 0.0 all-gather.2.cloned.1.call-start
  51.3 0.8 dynamic-slice
  52.1 0.1 tile.9
  52.2 0.1 reshape.44
  52.3 0.1 reshape.45
  52.4 0.1 fusion.17
  52.5 0.4 fusion.8
  52.9 13.0 %all-to-all-done = f32[4,1,32768]{2,1,0:T(1,128)S(1)} async-done(((f32[4,1,32768]{2,1,0:T(1,128)}), f32[4,1,32768]{2,1,0:T(1,128)S(1)}, u32[]{:S(2)}, u32[]{:S(2)}) %all-to-all-start) | async-done | bytes 524320 | tf_op jit(solution)/shard_map/all_to_all | solution.py:61
  65.8 0.5 broadcast.18
  66.3 2.2 %reduce = f32[4,32768]{1,0:T(4,128)S(1)} reduce(f32[4,1,32768]{2,1,0:T(1,128)S(1)} %all-to-all-done, f32[]{:T(128)} %broadcast.18), dimensions={1}, to_apply=%all_to_all.24.reduce_sub_computation | reduce | bytes 1048580 | tf_op jit(solution)/shard_map/all_to_all | solution.py:61
  68.5 28.0 %reshape.56 = f32[8192,4,4]{2,1,0:T(4,128)} reshape(f32[4,32768]{1,0:T(4,128)S(1)} %reduce) | data formatting | bytes 1048576
  96.5 13.4 %copy.30 = f32[4,4,4,2048]{3,0,2,1:T(4,128)S(1)} copy(f32[4,4,4,2048]{2,0,3,1:T(4,128)} %bitcast.69) | data formatting | bytes 1048576 | tf_op jit(solution)/shard_map/all_to_all | solution.py:61
  109.9 0.9 convolution_add_fusion.1
  110.8 1.1 convolution_add_fusion
  111.9 0.0 all-gather.2.cloned.1.call-update
  111.9 21.8 %all-gather.2.cloned.1.call-done = f32[16,16,2048]{2,1,0:T(8,128)} async-done(((f32[4,16,2048]{2,1,0:T(8,128)}), f32[16,16,2048]{2,1,0:T(8,128)}) %all-gather.2.cloned.1.call-update) | async-done | bytes 2097168 | tf_op jit(solution)/shard_map/all_gather | solution.py:69
  133.8 0.0 copy-done
  133.8 3.8 %fusion = f32[4,16,2048]{2,0,1:T(4,128)S(1)} fusion(f32[16,16,2048]{2,1,0:T(8,128)} %all-gather.2.cloned.1.call-done, f32[16,16]{1,0:T(8,128)S(1)} %copy-done, s32[]{:T(128)S(6)} %select_n.4), kind=kOutput, calls=%fused_computation.2 | convolution fusion | flops 25165824 | bytes 2623492 | tf_op jit(solution)/shard_map/oc,chw->ohw/dot_general | solution.py:66
  137.5 19.3 %all_to_all.33 = f32[4,16,2048]{2,0,1:T(4,128)S(1)} all-to-all(f32[4,16,2048]{2,0,1:T(4,128)S(1)} %fusion), channel_id=1, replica_groups=mesh['groups'=2,'band'=4,'chan'=4] {'band'}, dimensions={1} | all-to-all | bytes 1048576 | tf_op jit(solution)/shard_map/all_to_all | solution.py:72
  156.8 0.3 copy.34
  157.2 1.2 all_to_all.30
  (4 shorter events, 0.0 us)
Async XLA Ops:
  6.5 127.2 %copy-start = (f32[16,16]{1,0:T(8,128)S(1)}, f32[16,16]{1,0:T(8,128)}, u32[]{:S(2)}) copy-start(f32[16,16]{1,0:T(8,128)} %param.7) | copy-start | bytes 3076
  8.1 1.4 copy-start.1
  45.0 20.8 %all-to-all-start = ((f32[4,1,32768]{2,1,0:T(1,128)}), f32[4,1,32768]{2,1,0:T(1,128)S(1)}, u32[]{:S(2)}, u32[]{:S(2)}) async-start(f32[4,1,32768]{2,1,0:T(1,128)} %reshape.55), calls=%async_computation | async-start | bytes 1048576 | tf_op jit(solution)/shard_map/all_to_all | solution.py:61
  51.3 82.4 %all-gather.2.cloned.1.call-start = ((), (), s32[]{:S(2)}) async-start(), calls=%async_computation.2 | async-start | bytes 2621440 | tf_op jit(solution)/shard_map/all_gather | solution.py:69
Sparse Core Ops, SparseCore 0:
  112.1 21.6 all-gather.1
where the time goes:
time: 166 us; the launch traced here: 165 us
  local copies, waits for them, and re-layouts  81.1 us (49%)
  waiting for transfers between devices  34.8 us (21%)
  blocking collectives  19.3 us (12%)
  between operations  13.5 us (8%)
  matrix products  7.99 us (5%)
  starting transfers between devices  6.35 us (4%)
  other arithmetic  2.17 us (1%)
    unnamed x8, local copies, waits for them, and re-layouts  53.4 us
    all_gather x1, waiting for transfers between devices, on_device(): lax.all_gather(vertical, 'chan', axis=0, tiled=True)  21.8 us
    all_to_all x1, blocking collectives, on_device(): lax.all_to_all(blended, 'band', split_axis=1, concat_axis=2, tiled=True)  19.3 us
    all_to_all x2, local copies, waits for them, and re-layouts, on_device(): lax.all_to_all(across, 'band', split_axis=2, concat_axis=1, tiled=True)  13.9 us
    all_to_all x1, waiting for transfers between devices, on_device(): lax.all_to_all(across, 'band', split_axis=2, concat_axis=1, tiled=True)  13 us
    reshape x1, local copies, waits for them, and re-layouts, along_columns(): return result.reshape(channels, row_count, col_count)  8.62 us
    all_to_all x1, starting transfers between devices, on_device(): lax.all_to_all(across, 'band', split_axis=2, concat_axis=1, tiled=True)  6.35 us
    dot_general x1, matrix products, on_device(): jnp.einsum('oc,chw->ohw', own_mixing, lax.all_gather(vertical, 'chan', ax...  3.77 us
  transfers between devices with their start and end apart: 2, of which 2 were waited for; matrix products, arithmetic and copies ran while one was open for 1% of the time, Pallas kernels for 0%

commit v1 on v0

--- a/solution.py
+++ b/solution.py
@@ -58,7 +58,11 @@
 def on_device(slide_region, row_taps, column_taps, channel_mix):
     local_channels = slide_region.shape[0]
     across = along_columns(slide_region, row_taps)
-    column_band = lax.all_to_all(across, "band", split_axis=2, concat_axis=1, tiled=True)
+    next_value = jax.lax.axis_size("band")
+    w_next = jnp.split(across, next_value, 2)
+    f_next = jnp.stack(w_next, axis=0)
+    local_next = jax.lax.all_to_all(f_next, "band", split_axis=0, concat_axis=0)
+    column_band = jnp.concatenate(local_next, 1)
     first_channel = lax.axis_index("chan") * local_channels
     own_taps = lax.dynamic_slice_in_dim(column_taps, first_channel, local_channels, 0)
     vertical = along_rows(column_band, own_taps)

time: 166 us -> 89.8 us (0.54)
  local copies, waits for them, and re-layouts: 81.1 us -> 6.58 us
    unnamed x8 -> x6, local copies, waits for them, and re-layouts: 53.4 us -> 0.81 us
    all_to_all x2 -> x0, local copies, waits for them, and re-layouts: 13.9 us -> none  [on_device(): lax.all_to_all(across, 'band', split_axis=2, concat_axis=1, tiled=True)]
    reshape x1, local copies, waits for them, and re-layouts: 8.62 us -> 0.2 us  [along_columns(): return result.reshape(channels, row_count, col_count)]
    all_to_all x1 -> x0, other arithmetic: 2.17 us -> none  [on_device(): lax.all_to_all(across, 'band', split_axis=2, concat_axis=1, tiled=True)]
  transfers between devices with their start and end apart: 2 -> 2, of which waited for: 2 -> 2; matrix products, arithmetic and copies ran while one was open for 1% -> 2% of each run, Pallas kernels for 0% -> 0%
where the time goes in v1:
time: 89.8 us; the launch traced here: 89.5 us
  waiting for transfers between devices  34.8 us (39%)
  blocking collectives  19.3 us (21%)
  between operations  13.6 us (15%)
  matrix products  7.98 us (9%)
  local copies, waits for them, and re-layouts  6.58 us (7%)
  starting transfers between devices  6.35 us (7%)
  other arithmetic  0.92 us (1%)
    all_gather x1, waiting for transfers between devices, on_device(): lax.all_gather(vertical, 'chan', axis=0, tiled=True)  21.8 us
    all_to_all x1, blocking collectives, on_device(): lax.all_to_all(blended, 'band', split_axis=1, concat_axis=2, tiled=True)  19.3 us
    all_to_all x1, waiting for transfers between devices, on_device(): local_next = jax.lax.all_to_all(f_next, 'band', split_axis=0, concat_axis=0)  13 us
    all_to_all x1, starting transfers between devices, on_device(): local_next = jax.lax.all_to_all(f_next, 'band', split_axis=0, concat_axis=0)  6.35 us
    dot_general x1, matrix products, on_device(): jnp.einsum('oc,chw->ohw', own_mixing, lax.all_gather(vertical, 'chan', ax...  3.77 us
  transfers between devices with their start and end apart: 2, of which 2 were waited for; matrix products, arithmetic and copies ran while one was open for 2% of the time, Pallas kernels for 0%

profile of v1, /device:TPU:0, one launch (start us, length us, event | category | flops | bytes accessed | tf_op | source)
XLA Modules:
  0.0 89.5 jit_solution(15135651072376944974)
XLA Ops:
  6.5 0.0 copy-start
  6.5 0.7 pad_slice_fusion.4
  7.3 0.1 broadcast_bitcast_fusion
  7.4 0.7 copy.42
  8.1 0.1 slice.68
  8.1 0.0 copy-start.1
  8.2 1.0 %reshape.48 = f32[4,128,511]{2,1,0:T(8,128)S(1)} reshape(f32[4,65408]{1,0:T(4,128)S(1)} %slice.68) | data formatting | bytes 2093056 | tf_op jit(solution)/shard_map/reshape | solution.py:19
  9.2 0.1 slice_bitcast_fusion
  9.2 0.3 copy.17
  9.5 0.0 copy-done.1
  9.5 0.4 reshape.47
  9.9 0.6 fusion.4
  10.5 0.6 fusion.5
  11.2 0.6 fusion.3
  11.8 0.2 reshape.50
  12.0 0.2 copy_bitcast_fusion.2
  12.2 0.2 copy_bitcast_fusion
  12.4 0.9 %pad_maximum_fusion = f32[4,4,4,2048]{3,1,2,0:T(4,128)} fusion(f32[1,4,4,2048]{3,1,2,0:T(4,128)S(1)} %get-tuple-element.12, f32[1,4,4,2048]{3,1,2,0:T(4,128)S(1)} %get-tuple-element.13, f32[1,4,4,2048]{3,1,2,0:T(4,128)S(1)} %get-tuple-element.14, f32[1,4,4,2048]{3,1,2,0:T(4,128)S(1)} %get-tuple-element.15), kind=kLoop, calls=%fused_computation.12 | loop fusion | flops 393216 | bytes 1048576 | tf_op jit(solution)/shard_map/stack | solution.py:63
  13.3 6.3 %all-to-all-start = ((f32[4,4,4,2048]{3,1,2,0:T(4,128)}), f32[4,4,4,2048]{3,1,2,0:T(4,128)S(1)}, u32[]{:S(2)}, u32[]{:S(2)}) async-start(f32[4,4,4,2048]{3,1,2,0:T(4,128)} %pad_maximum_fusion), calls=%async_computation | async-start | bytes 1048576 | tf_op jit(solution)/shard_map/all_to_all | solution.py:64
  19.7 0.0 all-gather.2.cloned.1.call-start
  19.7 0.8 dynamic-slice
  20.4 0.1 tile.9
  20.5 0.1 reshape.45
  20.6 0.1 reshape.46
  20.7 0.1 fusion.18
  20.8 0.4 fusion.8
  21.2 13.0 %all-to-all-done = f32[4,4,4,2048]{3,1,2,0:T(4,128)S(1)} async-done(((f32[4,4,4,2048]{3,1,2,0:T(4,128)}), f32[4,4,4,2048]{3,1,2,0:T(4,128)S(1)}, u32[]{:S(2)}, u32[]{:S(2)}) %all-to-all-start) | async-done | bytes 524320 | tf_op jit(solution)/shard_map/all_to_all | solution.py:64
  34.1 0.8 convolution_add_fusion.1
  35.0 1.1 %convolution_add_fusion = f32[4,16,2048]{2,1,0:T(8,128)} fusion(f32[4,16,2048]{2,1,0:T(8,128)S(1)} %convolution_add_fusion.1, f32[4,16,16]{1,2,0:T(8,128)S(1)} %bitcast.79), kind=kOutput, calls=%fused_computation | convolution fusion | flops 25296896 | bytes 1052672 | tf_op jit(solution)/shard_map/ctiw,cij->ctjw/dot_general | solution.py:54
  36.1 0.0 all-gather.2.cloned.1.call-update
  36.2 21.8 %all-gather.2.cloned.1.call-done = f32[16,16,2048]{2,1,0:T(8,128)} async-done(((f32[4,16,2048]{2,1,0:T(8,128)}), f32[16,16,2048]{2,1,0:T(8,128)}) %all-gather.2.cloned.1.call-update) | async-done | bytes 2097168 | tf_op jit(solution)/shard_map/all_gather | solution.py:73
  58.0 0.0 copy-done
  58.0 3.8 %fusion = f32[4,16,2048]{2,0,1:T(4,128)S(1)} fusion(f32[16,16,2048]{2,1,0:T(8,128)} %all-gather.2.cloned.1.call-done, f32[16,16]{1,0:T(8,128)S(1)} %copy-done, s32[]{:T(128)S(6)} %select_n.4), kind=kOutput, calls=%fused_computation.2 | convolution fusion | flops 25165824 | bytes 2623492 | tf_op jit(solution)/shard_map/oc,chw->ohw/dot_general | solution.py:70
  61.8 19.3 %all_to_all.23 = f32[4,16,2048]{2,0,1:T(4,128)S(1)} all-to-all(f32[4,16,2048]{2,0,1:T(4,128)S(1)} %fusion), channel_id=1, replica_groups=mesh['groups'=2,'band'=4,'chan'=4] {'band'}, dimensions={1} | all-to-all | bytes 1048576 | tf_op jit(solution)/shard_map/all_to_all | solution.py:76
  81.0 0.3 copy.28
  81.4 1.2 %all_to_all.20 = f32[4,4,8192]{2,1,0:T(4,128)} reshape(f32[4,4,4,2048]{3,2,1,0:T(4,128)S(1)} %copy.28) | data formatting | bytes 1048576 | tf_op jit(solution)/shard_map/all_to_all | solution.py:76
  (5 shorter events, 0.1 us)
Async XLA Ops:
  6.5 51.5 %copy-start = (f32[16,16]{1,0:T(8,128)S(1)}, f32[16,16]{1,0:T(8,128)}, u32[]{:S(2)}) copy-start(f32[16,16]{1,0:T(8,128)} %param.7) | copy-start | bytes 3076
  8.1 1.4 %copy-start.1 = (f32[4,4,8192]{2,1,0:T(4,128)S(1)}, f32[4,4,8192]{2,1,0:T(4,128)}, u32[]{:S(2)}) copy-start(f32[4,4,8192]{2,1,0:T(4,128)} %param.4) | copy-start | bytes 1572868
  13.3 20.8 %all-to-all-start = ((f32[4,4,4,2048]{3,1,2,0:T(4,128)}), f32[4,4,4,2048]{3,1,2,0:T(4,128)S(1)}, u32[]{:S(2)}, u32[]{:S(2)}) async-start(f32[4,4,4,2048]{3,1,2,0:T(4,128)} %pad_maximum_fusion), calls=%async_computation | async-start | bytes 1048576 | tf_op jit(solution)/shard_map/all_to_all | solution.py:64
  19.7 38.3 %all-gather.2.cloned.1.call-start = ((), (), s32[]{:S(2)}) async-start(), calls=%async_computation.2 | async-start | bytes 2621440 | tf_op jit(solution)/shard_map/all_gather | solution.py:73
Sparse Core Ops, SparseCore 0:
  36.3 21.6 all-gather.1

commit v2 on v0

--- a/solution.py
+++ b/solution.py
@@ -63,12 +63,37 @@
     own_taps = lax.dynamic_slice_in_dim(column_taps, first_channel, local_channels, 0)
     vertical = along_rows(column_band, own_taps)
     own_mixing = lax.dynamic_slice_in_dim(channel_mix, first_channel, local_channels, 0)
+    devices, index, rows = (lax.axis_size("chan"), lax.axis_index("chan"), vertical.shape[0])
+    forward = [(i, (i + 1) % devices) for i in range(devices)]
+    backward = [(i, (i - 1) % devices) for i in range(devices)]
+    middle = devices // 2
+    from_left = from_right = vertical
     blended = jnp.einsum(
         "oc,chw->ohw",
-        own_mixing,
-        lax.all_gather(vertical, "chan", axis=0, tiled=True),
+        lax.dynamic_slice_in_dim(own_mixing, index * rows, vertical.shape[0], axis=1),
+        vertical,
         precision=precise,
     )
+    for step in range(1, middle + 1):
+        from_left = lax.ppermute(from_left, "chan", forward)
+        if step < devices - middle:
+            from_right = lax.ppermute(from_right, "chan", backward)
+            blended = blended + jnp.einsum(
+                "oc,chw->ohw",
+                lax.dynamic_slice_in_dim(
+                    own_mixing, (index + step) % devices * rows, from_right.shape[0], axis=1
+                ),
+                from_right,
+                precision=precise,
+            )
+        blended = blended + jnp.einsum(
+            "oc,chw->ohw",
+            lax.dynamic_slice_in_dim(
+                own_mixing, (index - step) % devices * rows, from_left.shape[0], axis=1
+            ),
+            from_left,
+            precision=precise,
+        )
     return lax.all_to_all(blended, "band", split_axis=1, concat_axis=2, tiled=True)
 
 

time: 166 us -> 147 us (0.89)
  between operations: 13.5 us -> 0.18 us
  waiting for transfers between devices: 34.8 us -> 28.2 us
  blocking collectives: 19.3 us -> 17.4 us
  starting transfers between devices: 6.35 us -> 8.24 us
    all_gather x1 -> x0, waiting for transfers between devices: 21.8 us -> none  [on_device(): lax.all_gather(vertical, 'chan', axis=0, tiled=True)]
    ppermute x0 -> x3, waiting for transfers between devices: none -> 15.3 us  [the longest x2 14.6 us: on_device(): from_left = lax.ppermute(from_left, 'chan', forward)]
    ppermute x0 -> x3, starting transfers between devices: none -> 1.89 us  [the longest x1 1.73 us: on_device(): from_right = lax.ppermute(from_right, 'chan', backward)]
    all_to_all x1, blocking collectives: 19.3 us -> 17.4 us  [on_device(): lax.all_to_all(blended, 'band', split_axis=1, concat_axis=2, tiled=True)]
    dot_general x1 -> x4, matrix products: 3.77 us -> 5.18 us  [the longest x2 2.61 us: on_device(): jnp.einsum('oc,chw->ohw', lax.dynamic_slice_in_dim(own_mixing, (index - s...]
    unnamed x8 -> x6, local copies, waits for them, and re-layouts: 53.4 us -> 53.4 us
  transfers between devices with their start and end apart: 2 -> 4, of which waited for: 2 -> 4; matrix products, arithmetic and copies ran while one was open for 1% -> 4% of each run, Pallas kernels for 0% -> 0%
where the time goes in v2:
time: 147 us
  local copies, waits for them, and re-layouts  82.3 us (56%)
  waiting for transfers between devices  28.2 us (19%)
  blocking collectives  17.4 us (12%)
  matrix products  8.33 us (6%)
  starting transfers between devices  8.24 us (6%)
  other arithmetic  2.17 us (1%)
    unnamed x6, local copies, waits for them, and re-layouts  53.4 us
    all_to_all x1, blocking collectives, on_device(): lax.all_to_all(blended, 'band', split_axis=1, concat_axis=2, tiled=True)  17.4 us
    ppermute x2, waiting for transfers between devices, on_device(): from_left = lax.ppermute(from_left, 'chan', forward)  14.6 us
    all_to_all x2, local copies, waits for them, and re-layouts, on_device(): lax.all_to_all(across, 'band', split_axis=2, concat_axis=1, tiled=True)  13.9 us
    all_to_all x1, waiting for transfers between devices, on_device(): lax.all_to_all(across, 'band', split_axis=2, concat_axis=1, tiled=True)  12.9 us
    reshape x1, local copies, waits for them, and re-layouts, along_columns(): return result.reshape(channels, row_count, col_count)  8.59 us
    all_to_all x1, starting transfers between devices, on_device(): lax.all_to_all(across, 'band', split_axis=2, concat_axis=1, tiled=True)  6.35 us
  transfers between devices with their start and end apart: 4, of which 4 were waited for; matrix products, arithmetic and copies ran while one was open for 4% of the time, Pallas kernels for 0%

profile of v2, /device:TPU:0, one launch (start us, length us, event | category | flops | bytes accessed | tf_op | source)
XLA Modules:
  0.0 146.9 jit_solution(13429245418236757437)
XLA Ops:
  0.0 0.0 copy-start
  0.0 1.4 reshape.46
  1.4 0.7 pad_slice_fusion.4
  2.1 0.1 broadcast_bitcast_fusion
  2.3 0.7 copy.48
  2.9 0.1 slice.68
  3.0 1.0 reshape.47
  4.0 0.1 slice_bitcast_fusion
  4.1 0.3 copy.26
  4.4 0.6 fusion.3
  5.0 0.6 fusion.2
  5.6 0.6 fusion.1
  6.3 8.6 %copy.41 = f32[4,4,64,128]{1,0,3,2:T(4,128)} copy(f32[4,4,64,128]{3,2,1,0:T(8,128)S(1)} %fusion.1) | data formatting | bytes 1048576 | tf_op jit(solution)/shard_map/reshape | solution.py:40
  14.8 24.6 %reshape.58 = f32[4,1,32768]{2,1,0:T(1,128)} reshape(f32[8192,4,4]{2,1,0:T(4,128)} %bitcast.75) | data formatting | bytes 1048576
  39.4 6.4 %all-to-all-start = ((f32[4,1,32768]{2,1,0:T(1,128)}), f32[4,1,32768]{2,1,0:T(1,128)S(1)}, u32[]{:S(2)}, u32[]{:S(2)}) async-start(f32[4,1,32768]{2,1,0:T(1,128)} %reshape.58), calls=%async_computation | async-start | bytes 1048576 | tf_op jit(solution)/shard_map/all_to_all | solution.py:61
  45.8 0.8 dynamic-slice
  46.6 0.1 tile.9
  46.7 0.1 reshape.44
  46.8 0.1 reshape.45
  46.9 0.1 fusion.24
  47.0 0.4 fusion.10
  47.3 12.9 %all-to-all-done = f32[4,1,32768]{2,1,0:T(1,128)S(1)} async-done(((f32[4,1,32768]{2,1,0:T(1,128)}), f32[4,1,32768]{2,1,0:T(1,128)S(1)}, u32[]{:S(2)}, u32[]{:S(2)}) %all-to-all-start) | async-done | bytes 524320 | tf_op jit(solution)/shard_map/all_to_all | solution.py:61
  60.3 0.5 broadcast.21
  60.8 2.2 %reduce = f32[4,32768]{1,0:T(4,128)S(1)} reduce(f32[4,1,32768]{2,1,0:T(1,128)S(1)} %all-to-all-done, f32[]{:T(128)} %broadcast.21), dimensions={1}, to_apply=%all_to_all.24.reduce_sub_computation | reduce | bytes 1048580 | tf_op jit(solution)/shard_map/all_to_all | solution.py:61
  63.0 28.0 %reshape.59 = f32[8192,4,4]{2,1,0:T(4,128)} reshape(f32[4,32768]{1,0:T(4,128)S(1)} %reduce) | data formatting | bytes 1048576
  91.0 13.4 %copy.31 = f32[4,4,4,2048]{3,1,2,0:T(4,128)S(1)} copy(f32[4,4,4,2048]{1,0,3,2:T(4,128)} %bitcast.76) | data formatting | bytes 1048576 | tf_op jit(solution)/shard_map/all_to_all | solution.py:61
  104.4 0.2 reshape.50
  104.6 0.6 convolution_add_fusion.4
  105.1 0.4 convolution_add_fusion.3
  105.5 0.1 collective-permute-start.1
  105.6 1.7 %collective-permute-start = (f32[4,16,2048]{2,1,0:T(8,128)S(1)}, f32[4,16,2048]{2,1,0:T(8,128)S(1)}, u32[]{:S(2)}, u32[]{:S(2)}) collective-permute-start(f32[4,16,2048]{2,1,0:T(8,128)S(1)} %convolution_add_fusion.3), channel_id=1, source_target_pairs={{0,3},{1,0},{2,1},{3,2},{4,7},{5,4},{6,5},{7,6},{8,11},{9,8},{10,9... | collective-permute-start | bytes 1572872 | tf_op jit(solution)/shard_map/ppermute | solution.py:80
  107.3 0.0 copy-done
  107.3 1.3 fusion.7
  108.6 9.4 %collective-permute-done.1 = f32[4,16,2048]{2,1,0:T(8,128)S(1)} collective-permute-done((f32[4,16,2048]{2,1,0:T(8,128)S(1)}, f32[4,16,2048]{2,1,0:T(8,128)S(1)}, u32[]{:S(2)}, u32[]{:S(2)}) %collective-permute-start.1) | collective-permute-done | bytes 524320 | tf_op jit(solution)/shard_map/ppermute | solution.py:78
  118.0 0.1 collective-permute-start.2
  118.1 0.7 collective-permute-done
  118.8 1.3 convolution_add_fusion.2
  120.1 1.3 convolution_add_fusion.1
  121.4 5.2 %collective-permute-done.2 = f32[4,16,2048]{2,1,0:T(8,128)S(1)} collective-permute-done((f32[4,16,2048]{2,1,0:T(8,128)S(1)}, f32[4,16,2048]{2,1,0:T(8,128)S(1)}, u32[]{:S(2)}, u32[]{:S(2)}) %collective-permute-start.2) | collective-permute-done | bytes 524320 | tf_op jit(solution)/shard_map/ppermute | solution.py:78
  126.6 1.3 convolution_add_fusion
  127.9 17.4 %all_to_all.33 = f32[4,16,2048]{2,0,1:T(4,128)S(1)} all-to-all(f32[4,16,2048]{2,0,1:T(4,128)S(1)} %convolution_add_fusion), channel_id=1, replica_groups=mesh['groups'=2,'band'=4,'chan'=4] {'band'}, dimensions={1} | all-to-all | bytes 1048576 | tf_op jit(solution)/shard_map/all_to_all | solution.py:97
  145.3 0.3 copy.37
  145.7 1.2 all_to_all.30
  (4 shorter events, 0.0 us)
Async XLA Ops:
  0.0 107.3 %copy-start = (f32[16,16]{1,0:T(8,128)S(1)}, f32[16,16]{1,0:T(8,128)}, u32[]{:S(2)}) copy-start(f32[16,16]{1,0:T(8,128)} %param.7) | copy-start | bytes 3076
  39.4 20.8 %all-to-all-start = ((f32[4,1,32768]{2,1,0:T(1,128)}), f32[4,1,32768]{2,1,0:T(1,128)S(1)}, u32[]{:S(2)}, u32[]{:S(2)}) async-start(f32[4,1,32768]{2,1,0:T(1,128)} %reshape.58), calls=%async_computation | async-start | bytes 1048576 | tf_op jit(solution)/shard_map/all_to_all | solution.py:61
  105.5 12.5 %collective-permute-start.1 = (f32[4,16,2048]{2,1,0:T(8,128)S(1)}, f32[4,16,2048]{2,1,0:T(8,128)S(1)}, u32[]{:S(2)}, u32[]{:S(2)}) collective-permute-start(f32[4,16,2048]{2,1,0:T(8,128)S(1)} %convolution_add_fusion.3), channel_id=1, source_target_pairs={{0,1},{1,2},{2,3},{3,0},{4,5},{5,6},{6,7},{7,4},{8,9},{9,10},{10,1... | collective-permute-start | bytes 1572872 | tf_op jit(solution)/shard_map/ppermute | solution.py:78
  105.6 13.2 %collective-permute-start = (f32[4,16,2048]{2,1,0:T(8,128)S(1)}, f32[4,16,2048]{2,1,0:T(8,128)S(1)}, u32[]{:S(2)}, u32[]{:S(2)}) collective-permute-start(f32[4,16,2048]{2,1,0:T(8,128)S(1)} %convolution_add_fusion.3), channel_id=1, source_target_pairs={{0,3},{1,0},{2,1},{3,2},{4,7},{5,4},{6,5},{7,6},{8,11},{9,8},{10,9... | collective-permute-start | bytes 1572872 | tf_op jit(solution)/shard_map/ppermute | solution.py:80
  118.0 8.6 %collective-permute-start.2 = (f32[4,16,2048]{2,1,0:T(8,128)S(1)}, f32[4,16,2048]{2,1,0:T(8,128)S(1)}, u32[]{:S(2)}, u32[]{:S(2)}) collective-permute-start(f32[4,16,2048]{2,1,0:T(8,128)S(1)} %collective-permute-done.1), channel_id=1, source_target_pairs={{0,1},{1,2},{2,3},{3,0},{4,5},{5,6},{6,7},{7,4},{8,9},{9,10},{10,1... | collective-permute-start | bytes 1572872 | tf_op jit(solution)/shard_map/ppermute | solution.py:78
